TPU v7x, 32 devices: a whole 2x2x4 slice. The times are simulated.
32 devices in a mesh: pole: 2 (over y), row: 8 (over z, x), col: 2 (over core).
Axes of the slice: x: 2, y: 2, z: 4, core: 2. Of those that a mesh axis runs over, the one named last changes fastest.
Arguments:
- known_inverse: float32 [16, 128, 1024], P('pole', 'col', 'row'), parts along dimension 0, may hold values from -1 to 3, as said below
- first_factor: float32 [2048, 512], P(('pole', 'row')), parts along dimension 0, may hold values from -0.5 to 0.5
- first_corner: float32 [1024, 512], P('pole'), parts along dimension 0, may hold values from -1 to 5, as said below
- first_ancestors: int32 [1024], P('pole'), parts along dimension 0, may hold values from 0 to 1023, as said below
- second_factor: float32 [2048, 512], P(('pole', 'row')), parts along dimension 0, may hold values from -0.75 to 0.75
- second_link: float32 [1024, 512], P('pole'), parts along dimension 0, may hold values from -0.25 to 0.25
- second_corner: float32 [1024, 512], P('pole', 'col'), parts along dimension 0, may hold values from -1 to 5, as said below
- second_ancestors: int32 [512], P('pole'), parts along dimension 0, may hold values from 0 to 1023, as said below
Outputs:
- first_column: float32 [2048, 512], P(('pole', 'row'), 'col'), parts along dimension 0
- first_diagonal: float32 [1024, 512], P('pole', 'col'), parts along dimension 0
- second_column: float32 [2048, 512], P(('pole', 'row'), 'col'), parts along dimension 0
- second_cross: float32 [1024, 512], P('pole', 'col'), parts along dimension 0
- second_diagonal: float32 [1024, 512], P('pole', 'col'), parts along dimension 0
There are 2 independent parts, one for each index of `pole`. A program takes and returns all parts, laid end to end along the dimension named above; each array names one. Nothing has to cross between parts.
Inputs may be any that keep to these rules, and one draw needn't show every extreme that they name: `known_inverse`: K is symmetric. `first_corner`: symmetric. `second_corner`: symmetric. `first_ancestors`: distinct row numbers; every block of 128 consecutive row numbers starting at a multiple of 128 holds at least one of them. `second_ancestors`: distinct row numbers, each of which is also in first_ancestors; every block of 128 consecutive row numbers starting at a multiple of 128 holds at least one of them.
All inputs are finite; a program needn't handle non-finite values.
Results may differ from a plain program's by a relative error of at most 0.000084.
Values sent between devices are 32-bit elements; how exact they have to be, the bound alone decides.
A program may use at most 128 MiB of HBM per device.

v0:
```python
import jax
import jax.numpy as jnp
from jax import lax
from jax.sharding import PartitionSpec as P

HIGH = lax.Precision.HIGHEST


def product(left, right):
    return jnp.dot(left, right, precision=HIGH, preferred_element_type=jnp.float32)


def transposed_product(left, right):
    return lax.dot_general(
        left, right, (((0,), (0,)), ((), ())), precision=HIGH, preferred_element_type=jnp.float32
    )


def local_mask(ancestors, row_start, block_rows):
    global_rows = row_start + jnp.arange(block_rows, dtype=jnp.int32)
    return jnp.any(ancestors[:, None] == global_rows[None, :], axis=0).astype(jnp.float32)[:, None]


def on_device(
    known_inverse,
    first_factor,
    first_corner,
    first_ancestors,
    second_factor,
    second_link,
    second_corner,
    second_ancestors,
):
    groups, share_rows, block_rows = known_inverse.shape
    half_width = second_corner.shape[1]
    col_index = lax.axis_index("col")
    row_start = lax.axis_index("row") * block_rows
    first_mask = local_mask(first_ancestors, row_start, block_rows)
    second_mask = local_mask(second_ancestors, row_start, block_rows)
    first_masked = first_factor * first_mask
    second_masked = second_factor * second_mask
    share_start = col_index * share_rows
    first_piece = lax.dynamic_slice_in_dim(first_masked, share_start, share_rows, 0)
    second_piece = lax.dynamic_slice_in_dim(second_masked, share_start, share_rows, 0)
    columns = known_inverse.reshape(groups * share_rows, block_rows)

    def add_piece(piece):
        return transposed_product(columns, piece)

    first_partial = add_piece(lax.all_gather(first_piece, "row", axis=0, tiled=True))
    second_partial = add_piece(lax.all_gather(second_piece, "row", axis=0, tiled=True))
    first_image = lax.psum_scatter(first_partial, "col", scatter_dimension=1, tiled=True)
    first_column = -(first_image * first_mask)
    first_full = lax.all_gather(first_column, "col", axis=1, tiled=True)
    diagonal_partial = transposed_product(first_masked, first_column)
    corner_half = lax.dynamic_slice_in_dim(first_corner, col_index * half_width, half_width, 1)
    first_diagonal = corner_half - lax.psum(diagonal_partial, "row")
    diagonal_full = lax.all_gather(first_diagonal, "col", axis=1, tiled=True)
    second_image = lax.psum_scatter(second_partial, "col", scatter_dimension=1, tiled=True)
    link_half = lax.dynamic_slice_in_dim(second_link, col_index * half_width, half_width, 1)
    second_column = -((second_image + product(first_full, link_half)) * second_mask)
    second_half = lax.dynamic_slice_in_dim(second_masked, col_index * half_width, half_width, 1)
    cross_partial = transposed_product(first_full, second_half)
    closing_partial = transposed_product(second_masked, second_column)
    cross_total, closing_total = lax.psum((cross_partial, closing_partial), "row")
    second_cross = -(cross_total + product(diagonal_full, link_half))
    second_diagonal = second_corner - closing_total - transposed_product(second_link, second_cross)
    return (first_column, first_diagonal, second_column, second_cross, second_diagonal)


def solution(mesh):
    return jax.shard_map(
        on_device,
        mesh=mesh,
        in_specs=(
            P("pole", "col", "row"),
            P(("pole", "row"), None),
            P("pole", None),
            P("pole"),
            P(("pole", "row"), None),
            P("pole", None),
            P("pole", "col"),
            P("pole"),
        ),
        out_specs=(
            P(("pole", "row"), "col"),
            P("pole", "col"),
            P(("pole", "row"), "col"),
            P("pole", "col"),
            P("pole", "col"),
        ),
        check_vma=False,
    )
```

profile of v0, /device:TPU:0, one launch (start us, length us, event | category | flops | bytes accessed | tf_op | source)
XLA Modules:
  0.0 233.3 jit_solution(5799603692559722448)
XLA Ops:
  7.3 0.7 copy-done.8
  8.2 1.0 broadcast_multiply_fusion.1
  9.2 0.7 constant_dynamic-slice_fusion.1
  10.0 0.6 copy-done.9
  10.8 0.7 constant_dynamic-slice_fusion
  11.5 42.2 %all-gather.4.cloned.1.call-done = f32[512,512]{1,0:T(8,128)} async-done(((f32[64,512]{1,0:T(8,128)}), f32[512,512]{1,0:T(8,128)}) %all-gather.4.cloned.1.call-update) | async-done | bytes 1048592 | tf_op jit(solution)/shard_map/all_gather | solution.py:50
  53.7 3.7 %convolution_bitcast_fusion.2 = f32[128,512]{0,1:T(8,128)} fusion(f32[512,512]{1,0:T(8,128)} %all-gather.4.cloned.1.call-done, f32[512,128]{1,0:T(8,128)S(1)} %bitcast.22), kind=kOutput, calls=%fused_computation.5 | convolution fusion | flops 402653184 | bytes 1572864 | tf_op jit(solution)/shard_map/dot_general | solution.py:14
  57.5 37.9 %all-gather.6.cloned.1.call-done = f32[512,512]{1,0:T(8,128)} async-done(((f32[64,512]{1,0:T(8,128)}), f32[512,512]{1,0:T(8,128)}) %all-gather.6.cloned.1.call-update) | async-done | bytes 1048592 | tf_op jit(solution)/shard_map/all_gather | solution.py:51
  95.4 3.7 %convolution_bitcast_fusion.1 = f32[128,512]{0,1:T(8,128)} fusion(f32[512,512]{1,0:T(8,128)} %all-gather.6.cloned.1.call-done, f32[512,128]{1,0:T(8,128)S(1)} %bitcast.23), kind=kOutput, calls=%fused_computation.4 | convolution fusion | flops 402653184 | bytes 1572864 | tf_op jit(solution)/shard_map/dot_general | solution.py:14
  99.2 5.5 %reduce-scatter.3.cloned.1.call-done = f32[128,256]{0,1:T(8,128)} async-done(((f32[128,512]{0,1:T(8,128)}), f32[128,256]{0,1:T(8,128)}) %reduce-scatter.3.cloned.1.call-update) | async-done | bytes 131088 | tf_op jit(solution)/shard_map/reduce_scatter | solution.py:52
  104.7 0.9 multiply_negate_fusion
  105.6 2.0 all_gather.14
  107.6 1.4 fusion.6
  109.0 1.4 fusion.11
  110.4 5.9 %reduce-scatter.5.cloned.1.call-done = f32[128,256]{0,1:T(8,128)} async-done(((f32[128,512]{0,1:T(8,128)}), f32[128,256]{0,1:T(8,128)}) %reduce-scatter.5.cloned.1.call-update) | async-done | bytes 131088 | tf_op jit(solution)/shard_map/reduce_scatter | solution.py:59
  116.3 1.9 fusion.3
  118.2 1.4 fusion.12
  119.7 91.4 %all-reduce.3.cloned.1.call-done = (f32[512,256]{1,0:T(8,128)}, f32[512,256]{1,0:T(8,128)}, f32[512,256]{1,0:T(8,128)}) async-done(((f32[512,256]{1,0:T(8,128)}, f32[512,256]{1,0:T(8,128)}, f32[512,256]{1,0:T(8,128)}), (f32[512,256]{1,0:T(8,128)}, f32[512,256]{1,0:T(8,128)}, f32[512,256]{1,0:T(8,128)})) %all-reduce.3.cloned.1.call-update) | async-done | bytes 1572880 | tf_op jit(solution)/shard_map/psum | solution.py:57
  211.1 1.9 dynamic-slice_subtract_fusion
  213.1 0.8 copy.19
  213.8 0.8 copy.20
  214.6 6.9 %all-gather.8.cloned.1.call-done = f32[512,512]{1,0:T(8,128)} async-done(((f32[512,256]{1,0:T(8,128)}), f32[512,512]{1,0:T(8,128)}) %all-gather.8.cloned.1.call-update) | async-done | bytes 1048592 | tf_op jit(solution)/shard_map/all_gather | solution.py:58
  221.5 2.3 fusion
  223.8 2.6 %fusion.1 = f32[512,256]{1,0:T(8,128)} fusion(f32[512,256]{1,0:T(8,128)S(1)} %fusion, f32[512,512]{1,0:T(8,128)S(1)} %copy-done, f32[512,256]{1,0:T(8,128)S(1)} %copy-done.3, f32[512,256]{1,0:T(8,128)S(1)} %copy-done.4), kind=kOutput, calls=%fused_computation.3 | convolution fusion | flops 805568512 | bytes 3145728 | tf_op jit(solution)/shard_map/dot_general | solution.py:14
  (36 shorter events, 0.8 us)
Async XLA Ops:
  7.2 109.1 %copy-start = (f32[512,512]{1,0:T(8,128)S(1)}, f32[512,512]{1,0:T(8,128)}, u32[]{:S(2)}) copy-start(f32[512,512]{1,0:T(8,128)} %param.13) | copy-start | bytes 3145732
  7.2 46.5 %all-gather.4.cloned.1.call-start = ((), (), s32[]{:S(2)}) async-start(), calls=%async_computation.2 | async-start | bytes 1179648 | tf_op jit(solution)/shard_map/all_gather | solution.py:50
  7.2 0.8 copy-start.8
  9.2 1.5 copy-start.6
  9.9 0.7 copy-start.9
  9.9 85.5 %all-gather.6.cloned.1.call-start = ((), (), s32[]{:S(2)}) async-start(), calls=%async_computation.4 | async-start | bytes 1179648 | tf_op jit(solution)/shard_map/all_gather | solution.py:51
  10.8 42.9 %copy-start.2 = (f32[8,64,128]{2,1,0:T(8,128)S(1)}, f32[8,64,128]{2,1,0:T(8,128)}, u32[]{:S(2)}) copy-start(f32[8,64,128]{2,1,0:T(8,128)} %param.8) | copy-start | bytes 786436
  11.5 93.2 %reduce-scatter.3.cloned.1.call-start = ((), (), s32[]{:S(2)}) async-start(), calls=%async_computation.3 | async-start | bytes 393216 | tf_op jit(solution)/shard_map/reduce_scatter | solution.py:52
  57.5 58.8 %reduce-scatter.5.cloned.1.call-start = ((), (), s32[]{:S(2)}) async-start(), calls=%async_computation.5 | async-start | bytes 393216 | tf_op jit(solution)/shard_map/reduce_scatter | solution.py:59
  99.2 111.9 %all-reduce.3.cloned.1.call-start = ((), (), s32[]{:S(2)}) async-start(), calls=%async_computation.7 | async-start | bytes 3145728 | tf_op jit(solution)/shard_map/psum | solution.py:57
  118.2 93.0 %copy-start.7 = (f32[512,512]{1,0:T(8,128)S(1)}, f32[512,512]{1,0:T(8,128)}, u32[]{:S(2)}) copy-start(f32[512,512]{1,0:T(8,128)} %param.10) | copy-start | bytes 3145732
  119.6 101.8 %all-gather.8.cloned.1.call-start = ((), (), s32[]{:S(2)}) async-start(), calls=%async_computation.6 | async-start | bytes 1572864 | tf_op jit(solution)/shard_map/all_gather | solution.py:58
  213.0 8.4 %copy-start.5 = (f32[512,256]{1,0:T(8,128)S(1)}, f32[512,256]{1,0:T(8,128)}, u32[]{:S(2)}) copy-start(f32[512,256]{1,0:T(8,128)} %get-tuple-element.16) | copy-start | bytes 1572868
  221.5 2.3 copy-start.3
  221.5 2.3 copy-start.4
  223.8 2.7 %copy-start.1 = (f32[512,256]{1,0:T(8,128)}, f32[512,256]{1,0:T(8,128)S(1)}, u32[]{:S(2)}) copy-start(f32[512,256]{1,0:T(8,128)S(1)} %fusion) | copy-start | bytes 1572868
Sparse Core Ops, SparseCore 0:
  10.7 42.9 all-gather.3
  56.4 38.9 all-gather.5
  98.2 6.4 reduce-scatter.2
  107.4 8.8 reduce-scatter.4
  120.6 90.5 all-reduce.2
  213.2 8.2 all-gather.7
where the time goes:
time: 234 us; the launch traced here: 233 us
  waiting for transfers between devices  190 us (81%)
  matrix products  18.5 us (8%)
  between operations  14.2 us (6%)
  local copies, waits for them, and re-layouts  4.25 us (2%)
  other arithmetic  4.23 us (2%)
    psum x1, waiting for transfers between devices, on_device(): first_diagonal = corner_half - lax.psum(diagonal_partial, 'row')  91.4 us
    all_gather x1, waiting for transfers between devices, on_device(): lax.all_gather(first_piece, 'row', axis=0, tiled=True)  42.2 us
    all_gather x1, waiting for transfers between devices, on_device(): lax.all_gather(second_piece, 'row', axis=0, tiled=True)  37.9 us
    dot_general x6, matrix products, transposed_product(): lax.dot_general(left, right, (((0,), (0,)), ((), ())), precision=HIGH, pr...  14.3 us
    all_gather x1, waiting for transfers between devices, on_device(): diagonal_full = lax.all_gather(first_diagonal, 'col', axis=1, tiled=True)  6.88 us
    reduce_scatter x1, waiting for transfers between devices, on_device(): lax.psum_scatter(second_partial, 'col', scatter_dimension=1, tiled=True)  5.86 us
    reduce_scatter x1, waiting for transfers between devices, on_device(): lax.psum_scatter(first_partial, 'col', scatter_dimension=1, tiled=True)  5.48 us
  transfers between devices with their start and end apart: 6, of which 6 were waited for; matrix products, arithmetic and copies ran while one was open for 6% of the time, Pallas kernels for 0%

commit v1 on v0

--- a/solution.py
+++ b/solution.py
@@ -54,7 +54,7 @@
     first_full = lax.all_gather(first_column, "col", axis=1, tiled=True)
     diagonal_partial = transposed_product(first_masked, first_column)
     corner_half = lax.dynamic_slice_in_dim(first_corner, col_index * half_width, half_width, 1)
-    first_diagonal = corner_half - lax.psum(diagonal_partial, "row")
+    first_diagonal = corner_half - jnp.sum(lax.all_gather(diagonal_partial, "row"), axis=0)
     diagonal_full = lax.all_gather(first_diagonal, "col", axis=1, tiled=True)
     second_image = lax.psum_scatter(second_partial, "col", scatter_dimension=1, tiled=True)
     link_half = lax.dynamic_slice_in_dim(second_link, col_index * half_width, half_width, 1)

time: 234 us -> 298 us (1.27)
  waiting for transfers between devices: 190 us -> 249 us
  other arithmetic: 4.23 us -> 9.18 us
    all_gather x0 -> x1, waiting for transfers between devices: none -> 71.7 us  [on_device(): lax.all_gather(diagonal_partial, 'row')]
    psum x1, waiting for transfers between devices: 91.4 us -> 74.8 us  [on_device(): lax.psum((cross_partial, closing_partial), 'row')]
    all_gather x1, waiting for transfers between devices: 6.88 us -> 10.8 us  [on_device(): diagonal_full = lax.all_gather(first_diagonal, 'col', axis=1, tiled=True)]
  transfers between devices with their start and end apart: 6 -> 7, of which waited for: 6 -> 7; matrix products, arithmetic and copies ran while one was open for 6% -> 8% of each run, Pallas kernels for 0% -> 0%
where the time goes in v1:
time: 298 us; the launch traced here: 297 us
  waiting for transfers between devices  249 us (84%)
  matrix products  19.9 us (7%)
  between operations  14.2 us (5%)
  other arithmetic  9.18 us (3%)
    psum x1, waiting for transfers between devices, on_device(): lax.psum((cross_partial, closing_partial), 'row')  74.8 us
    all_gather x1, waiting for transfers between devices, on_device(): lax.all_gather(diagonal_partial, 'row')  71.7 us
    all_gather x1, waiting for transfers between devices, on_device(): lax.all_gather(first_piece, 'row', axis=0, tiled=True)  41.2 us
    all_gather x1, waiting for transfers between devices, on_device(): lax.all_gather(second_piece, 'row', axis=0, tiled=True)  37.9 us
    dot_general x6, matrix products, transposed_product(): lax.dot_general(left, right, (((0,), (0,)), ((), ())), precision=HIGH, pr...  15.6 us
    all_gather x1, waiting for transfers between devices, on_device(): diagonal_full = lax.all_gather(first_diagonal, 'col', axis=1, tiled=True)  10.8 us
    reduce_scatter x1, waiting for transfers between devices, on_device(): lax.psum_scatter(second_partial, 'col', scatter_dimension=1, tiled=True)  7.14 us
  transfers between devices with their start and end apart: 7, of which 7 were waited for; matrix products, arithmetic and copies ran while one was open for 8% of the time, Pallas kernels for 0%

profile of v1, /device:TPU:0, one launch (start us, length us, event | category | flops | bytes accessed | tf_op | source)
XLA Modules:
  0.0 297.4 jit_solution(5994508977713043666)
XLA Ops:
  7.2 0.9 compare_reduce_fusion
  8.2 1.0 broadcast_multiply_fusion.1
  9.9 0.8 compare_reduce_fusion.1
  10.8 1.0 broadcast_multiply_fusion
  12.5 41.2 %all-gather.6.cloned.1.call-done = f32[512,512]{1,0:T(8,128)} async-done(((f32[64,512]{1,0:T(8,128)}), f32[512,512]{1,0:T(8,128)}) %all-gather.6.cloned.1.call-update) | async-done | bytes 1048592 | tf_op jit(solution)/shard_map/all_gather | solution.py:50
  53.7 3.8 %convolution_bitcast_fusion.2 = f32[128,512]{0,1:T(8,128)} fusion(f32[512,512]{1,0:T(8,128)} %all-gather.6.cloned.1.call-done, f32[512,128]{1,0:T(8,128)} %bitcast.24), kind=kOutput, calls=%fused_computation.5 | convolution fusion | flops 402653184 | bytes 1572864 | tf_op jit(solution)/shard_map/dot_general | solution.py:14
  57.6 37.9 %all-gather.8.cloned.1.call-done = f32[512,512]{1,0:T(8,128)} async-done(((f32[64,512]{1,0:T(8,128)}), f32[512,512]{1,0:T(8,128)}) %all-gather.8.cloned.1.call-update) | async-done | bytes 1048592 | tf_op jit(solution)/shard_map/all_gather | solution.py:51
  95.4 3.8 %convolution_bitcast_fusion.1 = f32[128,512]{0,1:T(8,128)} fusion(f32[512,512]{1,0:T(8,128)} %all-gather.8.cloned.1.call-done, f32[512,128]{1,0:T(8,128)} %bitcast.25), kind=kOutput, calls=%fused_computation.4 | convolution fusion | flops 402653184 | bytes 1572864 | tf_op jit(solution)/shard_map/dot_general | solution.py:14
  99.3 5.4 %reduce-scatter.3.cloned.1.call-done = f32[128,256]{0,1:T(8,128)} async-done(((f32[128,512]{0,1:T(8,128)}), f32[128,256]{0,1:T(8,128)}) %reduce-scatter.3.cloned.1.call-update) | async-done | bytes 131088 | tf_op jit(solution)/shard_map/reduce_scatter | solution.py:52
  104.7 0.9 multiply_negate_fusion
  105.6 1.4 fusion.11
  107.1 2.0 all_gather.22
  109.1 7.1 %reduce-scatter.5.cloned.1.call-done = f32[128,256]{0,1:T(8,128)} async-done(((f32[128,512]{0,1:T(8,128)}), f32[128,256]{0,1:T(8,128)}) %reduce-scatter.5.cloned.1.call-update) | async-done | bytes 131088 | tf_op jit(solution)/shard_map/reduce_scatter | solution.py:59
  116.3 1.9 fusion.3
  118.2 1.4 fusion.6
  119.5 1.4 fusion.12
  121.1 71.7 %all-gather.12.cloned.1.call-done = f32[4096,256]{1,0:T(8,128)} async-done(((f32[512,256]{1,0:T(8,128)}), f32[4096,256]{1,0:T(8,128)}) %all-gather.12.cloned.1.call-update) | async-done | bytes 4194320 | tf_op jit(solution)/shard_map/all_gather | solution.py:57
  192.8 2.6 reduce_sum.9
  195.3 1.9 dynamic-slice_subtract_fusion
  197.3 0.8 copy.19
  198.8 74.8 %all-reduce.3.cloned.1.call-done = (f32[512,256]{1,0:T(8,128)}, f32[512,256]{1,0:T(8,128)}) async-done(((f32[512,256]{1,0:T(8,128)}, f32[512,256]{1,0:T(8,128)}), (f32[512,256]{1,0:T(8,128)}, f32[512,256]{1,0:T(8,128)})) %all-reduce.3.cloned.1.call-update) | async-done | bytes 1048592 | tf_op jit(solution)/shard_map/psum | solution.py:65
  273.6 10.8 %all-gather.10.cloned.1.call-done = f32[512,512]{1,0:T(8,128)} async-done(((f32[512,256]{1,0:T(8,128)}), f32[512,512]{1,0:T(8,128)}) %all-gather.10.cloned.1.call-update) | async-done | bytes 1048592 | tf_op jit(solution)/shard_map/all_gather | solution.py:58
  284.4 2.3 fusion
  286.7 3.8 %fusion.1 = f32[512,256]{1,0:T(8,128)} fusion(f32[512,256]{1,0:T(8,128)S(1)} %fusion, f32[512,512]{1,0:T(8,128)S(1)} %copy-done, f32[512,256]{1,0:T(8,128)S(1)} %copy-done.2, f32[512,256]{1,0:T(8,128)} %get-tuple-element.16), kind=kOutput, calls=%fused_computation.3 | convolution fusion | flops 805568512 | bytes 3145728 | tf_op jit(solution)/shard_map/dot_general | solution.py:14
  (26 shorter events, 2.5 us)
Async XLA Ops:
  7.2 109.1 %copy-start = (f32[512,512]{1,0:T(8,128)S(1)}, f32[512,512]{1,0:T(8,128)}, u32[]{:S(2)}) copy-start(f32[512,512]{1,0:T(8,128)} %param.13) | copy-start | bytes 3145732
  7.2 46.5 %all-gather.6.cloned.1.call-start = ((), (), s32[]{:S(2)}) async-start(), calls=%async_computation.2 | async-start | bytes 1179648 | tf_op jit(solution)/shard_map/all_gather | solution.py:50
  9.9 85.5 %all-gather.8.cloned.1.call-start = ((), (), s32[]{:S(2)}) async-start(), calls=%async_computation.4 | async-start | bytes 1179648 | tf_op jit(solution)/shard_map/all_gather | solution.py:51
  12.5 92.2 %reduce-scatter.3.cloned.1.call-start = ((), (), s32[]{:S(2)}) async-start(), calls=%async_computation.3 | async-start | bytes 393216 | tf_op jit(solution)/shard_map/reduce_scatter | solution.py:52
  57.5 58.8 %reduce-scatter.5.cloned.1.call-start = ((), (), s32[]{:S(2)}) async-start(), calls=%async_computation.5 | async-start | bytes 393216 | tf_op jit(solution)/shard_map/reduce_scatter | solution.py:59
  99.2 93.5 %all-gather.12.cloned.1.call-start = ((), (), s32[]{:S(2)}) async-start(), calls=%async_computation.7 | async-start | bytes 4718592 | tf_op jit(solution)/shard_map/all_gather | solution.py:57
  107.1 166.5 %all-reduce.3.cloned.1.call-start = ((), (), s32[]{:S(2)}) async-start(), calls=%async_computation.8 | async-start | bytes 2097152 | tf_op jit(solution)/shard_map/psum | solution.py:65
  121.0 163.4 %all-gather.10.cloned.1.call-start = ((), (), s32[]{:S(2)}) async-start(), calls=%async_computation.6 | async-start | bytes 1572864 | tf_op jit(solution)/shard_map/all_gather | solution.py:58
  192.8 94.0 %copy-start.2 = (f32[512,256]{1,0:T(8,128)S(1)}, f32[512,256]{1,0:T(8,128)}, u32[]{:S(2)}) copy-start(f32[512,256]{1,0:T(8,128)} %param.14) | copy-start | bytes 1572868
  286.7 3.9 %copy-start.1 = (f32[512,256]{1,0:T(8,128)}, f32[512,256]{1,0:T(8,128)S(1)}, u32[]{:S(2)}) copy-start(f32[512,256]{1,0:T(8,128)S(1)} %fusion) | copy-start | bytes 1572868
Sparse Core Ops, SparseCore 0:
  10.7 42.9 all-gather.5
  56.4 38.9 all-gather.7
  98.2 6.4 reduce-scatter.2
  107.4 8.8 reduce-scatter.4
  118.8 73.8 all-gather.11
  196.7 76.7 all-reduce.2
  275.7 8.6 all-gather.9
